TPU v7x, 32 devices: a whole 2x2x4 slice. The times are simulated.
32 devices in a mesh: gx: 32 (over z, y, x, core).
Axes of the slice: x: 2, y: 2, z: 4, core: 2. Of those that a mesh axis runs over, the one named last changes fastest.
Arguments:
- fine: bfloat16 [64, 8192, 128], P(None, 'gx'), may hold values from -6 to 6
- pattern: int32 [8, 8192], P(None, 'gx'), may hold values from 0 to 3
- stencil: bfloat16 [3, 128, 128], replicated, may hold values from -0.3125 to 0.3125
- restrict: bfloat16 [8, 4, 128, 128], replicated, may hold values from -0.5 to 0.5
- coarse_inv: bfloat16 [8, 128, 128], replicated, may hold values from -0.5 to 0.5
Outputs:
- smoothed: float32 [64, 8192, 128], P(None, 'gx')
All inputs are finite; a program needn't handle non-finite values.
Results may differ from a plain program's by a relative error of at most 0.0046.
Values may be sent and summed in bfloat16 or wider, within the bound.
A program may use at most 128 MiB of HBM per device.

v0:
```python
import functools

import jax
import jax.numpy as jnp
from jax import lax
from jax.experimental import pallas as pl
from jax.experimental.pallas import tpu as pltpu
from jax.sharding import PartitionSpec as P

MESH = pl.DeviceIdType.MESH
F32 = jnp.float32
BF16 = jnp.bfloat16
TILE = 16
VMEM_LIMIT = 63 * 2**20


def round_up(value, unit):
    return -(-value // unit) * unit


class Plan:
    def __init__(self, devices, vectors, blocks, width, levels, kinds):
        self.devices, self.vectors, self.blocks = devices, vectors, blocks
        self.width, self.levels, self.kinds = width, levels, kinds
        all_blocks = devices * blocks
        self.spans, self.local_spans, self.counts, self.groups = [], [], [], []
        for level in range(levels):
            span = all_blocks // max(all_blocks // 4 ** (level + 1), 1)
            local = min(span, blocks)
            self.spans.append(span)
            self.local_spans.append(local)
            self.counts.append(blocks // local)
            self.groups.append(span // local)
        self.narrow = [l for l in range(levels) if self.counts[l] > 1]
        self.wide = [l for l in range(levels) if self.counts[l] == 1]
        self.crossing = [l for l in range(levels) if self.groups[l] > 1]
        self.padded = {l: round_up(self.counts[l], TILE) for l in self.narrow}
        self.offsets, at = {}, 0
        for l in self.narrow:
            self.offsets[l] = at
            at += kinds * self.padded[l]
        self.narrow_rows = at
        self.wide_used = len(self.wide) * kinds + 2
        self.wide_rows = round_up(self.wide_used, TILE)


def wide_rows_onehot(plan, pattern, rows_axis):
    shape = (plan.wide_rows, plan.blocks) if rows_axis == 0 else (plan.blocks, plan.wide_rows)
    row = lax.broadcasted_iota(jnp.int32, shape, rows_axis)
    block = lax.broadcasted_iota(jnp.int32, shape, 1 - rows_axis)
    base = len(plan.wide) * plan.kinds
    hit = ((row == base) & (block == 0)) | ((row == base + 1) & (block == plan.blocks - 1))
    for position, level in enumerate(plan.wide):
        kinds = pattern[level : level + 1, :] if rows_axis == 0 else pattern[:, level : level + 1]
        first = position * plan.kinds
        inside = (row >= first) & (row < first + plan.kinds)
        hit = hit | (inside & (row - first == kinds))
    return hit.astype(F32).astype(BF16)


def narrow_onehot(plan, pattern, level, rows_axis):
    padded = plan.padded[level]
    rows = plan.kinds * padded
    shape = (rows, plan.blocks) if rows_axis == 0 else (plan.blocks, rows)
    row = lax.broadcasted_iota(jnp.int32, shape, rows_axis)
    block = lax.broadcasted_iota(jnp.int32, shape, 1 - rows_axis)
    kinds = pattern[level : level + 1, :] if rows_axis == 0 else pattern[:, level : level + 1]
    target = kinds * padded + block // plan.local_spans[level]
    return (row == target).astype(F32).astype(BF16)


def exchange_kernel(plan, chunk, pattern_ref, fine_hbm, restrict_hbm, inverse_hbm, lifted_hbm, wide_hbm, beside_ref,
                    fine_ref, restrict_ref, inverse_ref, lifted_ref, wide_ref, wide_f32, wide_onehot, onehot, few,
                    grouped, rows, coarse_ref, halo_ref,
                    from_group, to_column, from_column, to_group, back,
                    fine_sem, weight_sem, lifted_sem, wide_sem, group_send, group_recv,
                    column_send, column_recv, back_send, back_recv, halo_send, halo_recv):
    width, kinds = plan.width, plan.kinds
    steps = plan.vectors // chunk
    devices = plan.devices
    near = plan.groups[plan.crossing[0]]
    far = devices // near
    local = len(plan.wide) - len(plan.crossing)
    crossing = len(plan.crossing)
    part = plan.vectors // near
    me = lax.axis_index("gx")
    mine = lax.rem(me, near)
    place = me // near

    def chunk_of(step):
        return pl.ds(pl.multiple_of(step * chunk, chunk), chunk)

    def fine_copy(step):
        return pltpu.make_async_copy(fine_hbm.at[chunk_of(step)], fine_ref.at[chunk_of(step)], fine_sem.at[step])

    def lifted_copy(step):
        return pltpu.make_async_copy(lifted_ref.at[chunk_of(step)], lifted_hbm.at[chunk_of(step)], lifted_sem.at[step])

    weight_copies = [
        pltpu.make_async_copy(restrict_hbm, restrict_ref, weight_sem.at[0]),
        pltpu.make_async_copy(inverse_hbm, inverse_ref, weight_sem.at[1]),
    ]
    for step in range(steps):
        fine_copy(step).start()
    for copy in weight_copies:
        copy.start()

    def group_peer(apart):
        return place * near + lax.rem(mine + apart, near)

    def column_peer(apart):
        return lax.rem(place + apart, far) * near + mine

    nexts = lax.rem(me + 1, devices)
    previous = lax.rem(me + devices - 1, devices)
    barrier = pltpu.get_barrier_semaphore()
    peers = [group_peer(a) for a in range(1, near)] + [column_peer(a) for a in range(1, far)] + [nexts, previous]
    for peer in peers:
        pl.semaphore_signal(barrier, inc=1, device_id=(peer,), device_id_type=MESH)

    wide_onehot[...] = wide_rows_onehot(plan, pattern_ref[...], 0)

    def gather_wide(step, _):
        fine_copy(step).wait()
        here = chunk_of(step)
        for first in range(0, chunk, 2):
            at = step * chunk + first
            both = jnp.concatenate([fine_ref[at], fine_ref[at + 1]], axis=1)
            both = jnp.dot(wide_onehot[...], both, preferred_element_type=F32)
            few[first] = both[:, :width]
            few[first + 1] = both[:, width:]
        for row in range(plan.wide_used):
            rows[row, here, :] = few[:, row, :].astype(BF16)
        return 0

    lax.fori_loop(0, steps, gather_wide, 0)
    for copy in weight_copies:
        copy.wait()
    for position, level in enumerate(plan.wide):
        first = position * kinds
        joined = jnp.concatenate([rows[first + kind] for kind in range(kinds)], axis=1)
        coarse = jnp.dot(joined, restrict_ref[level], preferred_element_type=F32)
        coarse_ref[position] = (coarse * plan.spans[level] ** (-0.5)).astype(BF16)
    base = len(plan.wide) * kinds
    halo_ref[0] = rows[base]
    halo_ref[1] = rows[base + 1]

    pl.semaphore_wait(barrier, len(peers))

    def part_of(index):
        return pl.ds(pl.multiple_of(index * part, part), part)

    copies = []
    for apart in range(1, near):
        theirs = lax.rem(mine + apart, near)
        copies.append(pltpu.make_async_remote_copy(
            src_ref=coarse_ref.at[pl.ds(local, crossing), part_of(theirs), :],
            dst_ref=from_group.at[apart],
            send_sem=group_send.at[apart], recv_sem=group_recv.at[apart],
            device_id=(group_peer(apart),), device_id_type=MESH))
    halo_copies = []
    for side, peer in ((0, previous), (1, nexts)):
        halo_copies.append(pltpu.make_async_remote_copy(
            src_ref=halo_ref.at[side], dst_ref=beside_ref.at[1 - side],
            send_sem=halo_send.at[side], recv_sem=halo_recv.at[1 - side],
            device_id=(peer,), device_id_type=MESH))
    for copy in copies + halo_copies:
        copy.start()

    for level in plan.narrow:
        onehot[pl.ds(plan.offsets[level], kinds * plan.padded[level]), :] = narrow_onehot(
            plan, pattern_ref[...], level, 0)

    def narrow(step, _):
        here = chunk_of(step)
        for first in range(0, chunk, 2):
            at = step * chunk + first
            both = jnp.concatenate([fine_ref[at], fine_ref[at + 1]], axis=1)
            both = jnp.dot(onehot[...], both, preferred_element_type=F32).astype(BF16)
            grouped[first] = both[:, :width]
            grouped[first + 1] = both[:, width:]
        for level in plan.narrow:
            padded = plan.padded[level]
            slices = [pl.ds(plan.offsets[level] + kind * padded, padded) for kind in range(kinds)]
            joined = jnp.concatenate(
                [grouped[:, tile, :].reshape(chunk * padded, width) for tile in slices], axis=1)
            coarse = jnp.dot(joined, restrict_ref[level], preferred_element_type=F32)
            rounded = (coarse * plan.spans[level] ** (-0.5)).astype(BF16)
            solved = jnp.dot(rounded, inverse_ref[level], preferred_element_type=F32).astype(BF16)
            lifted = lax.dot_general(
                solved, restrict_ref[level], (((1,), (1,)), ((), ())), preferred_element_type=F32).astype(BF16)
            for kind, tile in enumerate(slices):
                lifted_ref[here, tile, :] = lifted[:, kind * width : (kind + 1) * width].reshape(chunk, padded, width)
        lifted_copy(step).start()
        return 0

    def lift_wide(position, rounded):
        level = plan.wide[position]
        solved = jnp.dot(rounded, inverse_ref[level], preferred_element_type=F32).astype(BF16)
        lifted = lax.dot_general(
            solved, restrict_ref[level], (((1,), (1,)), ((), ())), preferred_element_type=F32)
        for kind in range(kinds):
            wide_f32[:, position * kinds + kind, :] = lifted[:, kind * width : (kind + 1) * width]

    first_stop = steps // 4
    second_stop = steps - max(steps // 4, 1)
    lax.fori_loop(0, first_stop, narrow, 0)

    total = coarse_ref[pl.ds(local, crossing), part_of(mine), :].astype(F32)
    for apart, copy in enumerate(copies, 1):
        copy.wait_recv()
        total = total + from_group[apart].astype(F32)
    to_column[...] = total.astype(BF16)

    column_copies = []
    for apart in range(1, far):
        column_copies.append(pltpu.make_async_remote_copy(
            src_ref=to_column.at[pl.ds(1, crossing - 1)], dst_ref=from_column.at[apart],
            send_sem=column_send.at[apart], recv_sem=column_recv.at[apart],
            device_id=(column_peer(apart),), device_id_type=MESH))
    for copy in column_copies:
        copy.start()

    for row in range(plan.wide_used, plan.wide_rows):
        wide_f32[:, row, :] = jnp.zeros((plan.vectors, width), F32)
    for position in range(local):
        lift_wide(position, coarse_ref[position])
    lax.fori_loop(first_stop, second_stop, narrow, 0)

    to_group[0] = to_column[0]
    sums = [to_column[index].astype(F32) for index in range(crossing)]
    for apart, copy in enumerate(column_copies, 1):
        copy.wait_recv()
        source = lax.rem(place + far - apart, far)
        for index in range(1, crossing):
            reach = plan.groups[plan.crossing[index]] // near
            keep = (source // reach == place // reach).astype(F32)
            sums[index] = sums[index] + keep * from_column[apart, index - 1].astype(F32)
    for index in range(1, crossing):
        to_group[index] = sums[index].astype(BF16)

    back_copies = []
    for apart in range(1, near):
        back_copies.append(pltpu.make_async_remote_copy(
            src_ref=to_group, dst_ref=back.at[apart],
            send_sem=back_send.at[apart], recv_sem=back_recv.at[apart],
            device_id=(group_peer(apart),), device_id_type=MESH))
    for copy in back_copies:
        copy.start()

    lax.fori_loop(second_stop, steps, narrow, 0)
    for copy in halo_copies:
        copy.wait_recv()
    for copy in copies:
        copy.wait_send()
    coarse_ref[pl.ds(local, crossing), part_of(mine), :] = to_group[...]
    for apart, copy in enumerate(back_copies, 1):
        copy.wait_recv()
        source = lax.rem(mine + near - apart, near)
        coarse_ref[pl.ds(local, crossing), part_of(source), :] = back[apart]
    for position in range(local, len(plan.wide)):
        lift_wide(position, coarse_ref[position])
    wide_ref[...] = wide_f32[...].astype(BF16)
    wide_copy = pltpu.make_async_copy(wide_ref, wide_hbm, wide_sem)
    wide_copy.start()
    for step in range(steps):
        lifted_copy(step).wait()
    for copy in halo_copies + column_copies + back_copies:
        copy.wait_send()
    wide_copy.wait()


def final_kernel(plan, chunk, pattern_ref, beside_ref, stencil_ref,
                 fine_ref, lifted_ref, wide_ref, out_ref, spread, halo, before, after):
    step = pl.program_id(0)
    width, blocks = plan.width, plan.blocks

    @pl.when(step == 0)
    def _():
        turned = pattern_ref[...].T
        for level in plan.narrow:
            columns = pl.ds(plan.offsets[level], plan.kinds * plan.padded[level])
            spread[:, columns] = narrow_onehot(plan, turned, level, 1)
        spread[:, pl.ds(plan.narrow_rows, plan.wide_rows)] = wide_rows_onehot(plan, turned, 1)
        halo[0] = jnp.dot(beside_ref[0], stencil_ref[0], preferred_element_type=F32)
        halo[1] = jnp.dot(beside_ref[1], stencil_ref[2], preferred_element_type=F32)

    stencils = jnp.concatenate([stencil_ref[0], stencil_ref[1], stencil_ref[2]], axis=1)
    for first in range(0, chunk, 2):
        tables = [jnp.concatenate([lifted_ref[first + slot], wide_ref[first + slot]], axis=0) for slot in range(2)]
        both = jnp.dot(spread[...], jnp.concatenate(tables, axis=1), preferred_element_type=F32)
        for slot in range(2):
            vector = pl.ds(step * chunk + first + slot, 1)
            three = jnp.dot(fine_ref[first + slot], stencils, preferred_element_type=F32)
            before[slot, pl.ds(7, 1), :] = halo[0, vector, :]
            before[slot, pl.ds(8, blocks), :] = three[:, :width]
            after[slot, pl.ds(0, blocks), :] = three[:, 2 * width :]
            after[slot, pl.ds(blocks, 1), :] = halo[1, vector, :]
            result = both[:, slot * width : (slot + 1) * width] + three[:, width : 2 * width]
            result = result + before[slot, pl.ds(7, blocks), :]
            out_ref[first + slot] = result + after[slot, pl.ds(1, blocks), :]


def whole(ndim_shape):
    return pl.BlockSpec(ndim_shape, lambda *_: (0,) * len(ndim_shape))


def shards(fine, pattern, stencil, restrict, coarse_inv):
    devices = lax.axis_size("gx")
    vectors, blocks, width = fine.shape
    levels, kinds = restrict.shape[:2]
    plan = Plan(devices, vectors, blocks, width, levels, kinds)
    stacked = restrict.reshape(levels, kinds * width, width)
    wide_count = len(plan.wide)
    params = pltpu.CompilerParams(dimension_semantics=("arbitrary",), vmem_limit_bytes=VMEM_LIMIT)
    chunk = 16
    steps = vectors // chunk
    near = plan.groups[plan.crossing[0]]
    far = devices // near
    crossing = len(plan.crossing)
    part = vectors // near
    vmem = pl.BlockSpec(memory_space=pltpu.VMEM)
    hbm = pl.BlockSpec(memory_space=pl.ANY)
    dma = pltpu.SemaphoreType.DMA
    lifted, wide, beside = pl.pallas_call(
        functools.partial(exchange_kernel, plan, chunk),
        out_shape=(
            jax.ShapeDtypeStruct((vectors, plan.narrow_rows, width), BF16),
            jax.ShapeDtypeStruct((vectors, plan.wide_rows, width), BF16),
            jax.ShapeDtypeStruct((2, vectors, width), BF16),
        ),
        in_specs=[vmem, hbm, hbm, hbm],
        out_specs=(hbm, hbm, vmem),
        scratch_shapes=[
            pltpu.VMEM(fine.shape, BF16),
            pltpu.VMEM(stacked.shape, BF16),
            pltpu.VMEM(coarse_inv.shape, BF16),
            pltpu.VMEM((vectors, plan.narrow_rows, width), BF16),
            pltpu.VMEM((vectors, plan.wide_rows, width), BF16),
            pltpu.VMEM((vectors, plan.wide_rows, width), F32),
            pltpu.VMEM((plan.wide_rows, blocks), BF16),
            pltpu.VMEM((plan.narrow_rows, blocks), BF16),
            pltpu.VMEM((chunk, plan.wide_rows, width), F32),
            pltpu.VMEM((chunk, plan.narrow_rows, width), BF16),
            pltpu.VMEM((plan.wide_used, vectors, width), BF16),
            pltpu.VMEM((wide_count, vectors, width), BF16),
            pltpu.VMEM((2, vectors, width), BF16),
            pltpu.VMEM((near, crossing, part, width), BF16),
            pltpu.VMEM((crossing, part, width), BF16),
            pltpu.VMEM((far, crossing - 1, part, width), BF16),
            pltpu.VMEM((crossing, part, width), BF16),
            pltpu.VMEM((near, crossing, part, width), BF16),
            dma((steps,)), dma((2,)), dma((steps,)), dma,
            dma((near,)), dma((near,)), dma((far,)), dma((far,)), dma((near,)), dma((near,)), dma((2,)), dma((2,)),
        ],
        compiler_params=pltpu.CompilerParams(
            collective_id=0, has_side_effects=True, vmem_limit_bytes=VMEM_LIMIT),
        name="exchange",
    )(pattern, fine, stacked, coarse_inv)

    last = 8
    return pl.pallas_call(
        functools.partial(final_kernel, plan, last),
        grid=(vectors // last,),
        out_shape=jax.ShapeDtypeStruct(fine.shape, F32),
        in_specs=[
            whole(pattern.shape), whole(beside.shape), whole(stencil.shape),
            pl.BlockSpec((last, blocks, width), lambda i: (i, 0, 0)),
            pl.BlockSpec((last, plan.narrow_rows, width), lambda i: (i, 0, 0)),
            pl.BlockSpec((last, plan.wide_rows, width), lambda i: (i, 0, 0)),
        ],
        out_specs=pl.BlockSpec((last, blocks, width), lambda i: (i, 0, 0)),
        scratch_shapes=[
            pltpu.VMEM((blocks, plan.narrow_rows + plan.wide_rows), BF16),
            pltpu.VMEM((2, vectors, width), F32),
            pltpu.VMEM((2, blocks + 8, width), F32),
            pltpu.VMEM((2, blocks + 8, width), F32),
        ],
        compiler_params=params,
        name="final",
    )(pattern, beside, stencil, fine, lifted, wide)


def solution(mesh):
    in_specs = (P(None, "gx", None), P(None, "gx"), P(), P(), P())
    out_specs = P(None, "gx", None)
    return jax.shard_map(shards, mesh=mesh, in_specs=in_specs, out_specs=out_specs, check_vma=False)
```

profile of v0, /device:TPU:0, one launch (start us, length us, event | category | flops | bytes accessed | tf_op | source)
XLA Modules:
  0.0 33.5 jit_solution(3395085588204491096)
XLA Ops:
  0.0 20.3 %exchange.1 = (bf16[64,384,128]{2,1,0:T(8,128)(2,1)}, bf16[64,32,128]{2,1,0:T(8,128)(2,1)}, bf16[2,64,128]{2,1,0:T(8,128)(2,1)}) custom-call(s32[8,256]{1,0:T(8,128)} %pattern_ref.3, bf16[64,256,128]{2,1,0:T(8,128)(2,1)} %fine_ref.1, bf16[8,512,128]{2,1,0:T(8,128)(2,1)} %bitcast.1, bf16[8,128,128]{2,1,0:T(8,128)(2,1)} %inverse_hbm.1), custom_call_target="tpu_custom_call" | custom-call | tf_op jit(solution)/shard_map/exchange/pallas_call | solution.py:325
  20.3 13.2 %final.1 = f32[64,256,128]{2,1,0:T(8,128)} custom-call(s32[8,256]{1,0:T(8,128)} %pattern_ref.3, bf16[2,64,128]{2,1,0:T(8,128)(2,1)} %get-tuple-element.8.beside_ref, bf16[3,128,128]{2,1,0:T(8,128)(2,1)} %stencil_ref.1, bf16[64,256,128]{2,1,0:T(8,128)(2,1)} %fine_ref.1, bf16[64,384,128]{2,1,0:T(8,128)(2,1)} %get-tuple-element.9.lifted_ref, ...), custom_call_target="tpu_custom_call" | custom-call | tf_op jit(solution)/shard_map/final/pallas_call | solution.py:362
where the time goes:
time: 33.9 us; the launch traced here: 33.5 us
  Pallas kernels  33.5 us (99%)
    pallas_call x1, Pallas kernels, shards(): pl.pallas_call(functools.partial(exchange_kernel, plan, chunk), out_shape...  20.3 us
    pallas_call x1, Pallas kernels, shards(): pl.pallas_call(functools.partial(final_kernel, plan, last), grid=(vectors...  13.2 us

commit v1 on v0

--- a/solution.py
+++ b/solution.py
@@ -11,7 +11,7 @@
 F32 = jnp.float32
 BF16 = jnp.bfloat16
 TILE = 16
-VMEM_LIMIT = 63 * 2**20
+VMEM_LIMIT = 30 * 2**20
 
 
 def round_up(value, unit):
@@ -68,14 +68,19 @@
     target = kinds * padded + block // plan.local_spans[level]
     return (row == target).astype(F32).astype(BF16)
 
-
-def exchange_kernel(plan, chunk, pattern_ref, fine_hbm, restrict_hbm, inverse_hbm, lifted_hbm, wide_hbm, beside_ref,
-                    fine_ref, restrict_ref, inverse_ref, lifted_ref, wide_ref, wide_f32, wide_onehot, onehot, few,
-                    grouped, rows, coarse_ref, halo_ref,
+PITCH = 40
+
+
+def exchange_kernel(plan, chunk, pattern_hbm, fine_hbm, restrict_hbm, inverse_hbm, stencil_hbm,
+                    table_ref, level0_ref, spread_ref,
+                    pattern_ref, fine_ref, restrict_ref, inverse_ref, stencil_ref, wide_f32, wide_onehot, onehot, few,
+                    grouped, rows, coarse_ref, halo_ref, beside_ref, before, after,
                     from_group, to_column, from_column, to_group, back,
-                    fine_sem, weight_sem, lifted_sem, wide_sem, group_send, group_recv,
+                    fine_sem, weight_sem, group_send, group_recv,
                     column_send, column_recv, back_send, back_recv, halo_send, halo_recv):
-    width, kinds = plan.width, plan.kinds
+    width, kinds, blocks = plan.width, plan.kinds, plan.blocks
+    load = 16
+    loads = plan.vectors // load
     steps = plan.vectors // chunk
     devices = plan.devices
     near = plan.groups[plan.crossing[0]]
@@ -91,18 +96,24 @@
         return pl.ds(pl.multiple_of(step * chunk, chunk), chunk)
 
     def fine_copy(step):
-        return pltpu.make_async_copy(fine_hbm.at[chunk_of(step)], fine_ref.at[chunk_of(step)], fine_sem.at[step])
-
-    def lifted_copy(step):
-        return pltpu.make_async_copy(lifted_ref.at[chunk_of(step)], lifted_hbm.at[chunk_of(step)], lifted_sem.at[step])
-
+        here = pl.ds(step * load, load)
+        return pltpu.make_async_copy(fine_hbm.at[here], fine_ref.at[here], fine_sem.at[step])
+
+    wide_first = plan.wide[0]
+    wide_weights = pl.ds(wide_first, len(plan.wide))
     weight_copies = [
-        pltpu.make_async_copy(restrict_hbm, restrict_ref, weight_sem.at[0]),
-        pltpu.make_async_copy(inverse_hbm, inverse_ref, weight_sem.at[1]),
+        pltpu.make_async_copy(restrict_hbm.at[wide_weights], restrict_ref.at[wide_weights], weight_sem.at[0]),
+        pltpu.make_async_copy(restrict_hbm.at[pl.ds(0, wide_first)], restrict_ref.at[pl.ds(0, wide_first)], weight_sem.at[1]),
+        pltpu.make_async_copy(inverse_hbm, inverse_ref, weight_sem.at[2]),
+        pltpu.make_async_copy(stencil_hbm, stencil_ref, weight_sem.at[3]),
     ]
-    for step in range(steps):
+    pattern_copy = pltpu.make_async_copy(pattern_hbm, pattern_ref, weight_sem.at[4])
+    pattern_copy.start()
+    for step in range(loads - 1):
         fine_copy(step).start()
-    for copy in weight_copies:
+    weight_copies[0].start()
+    fine_copy(loads - 1).start()
+    for copy in weight_copies[1:]:
         copy.start()
 
     def group_peer(apart):
@@ -118,24 +129,21 @@
     for peer in peers:
         pl.semaphore_signal(barrier, inc=1, device_id=(peer,), device_id_type=MESH)
 
+    pattern_copy.wait()
     wide_onehot[...] = wide_rows_onehot(plan, pattern_ref[...], 0)
 
-    def gather_wide(step, _):
+    for step in range(loads):
         fine_copy(step).wait()
-        here = chunk_of(step)
-        for first in range(0, chunk, 2):
-            at = step * chunk + first
+        here = pl.ds(step * load, load)
+        for first in range(0, load, 2):
+            at = step * load + first
             both = jnp.concatenate([fine_ref[at], fine_ref[at + 1]], axis=1)
             both = jnp.dot(wide_onehot[...], both, preferred_element_type=F32)
-            few[first] = both[:, :width]
-            few[first + 1] = both[:, width:]
+            few[first, pl.ds(0, plan.wide_rows), :] = both[:, :width]
+            few[first + 1, pl.ds(0, plan.wide_rows), :] = both[:, width:]
         for row in range(plan.wide_used):
             rows[row, here, :] = few[:, row, :].astype(BF16)
-        return 0
-
-    lax.fori_loop(0, steps, gather_wide, 0)
-    for copy in weight_copies:
-        copy.wait()
+    weight_copies[0].wait()
     for position, level in enumerate(plan.wide):
         first = position * kinds
         joined = jnp.concatenate([rows[first + kind] for kind in range(kinds)], axis=1)
@@ -170,15 +178,33 @@
     for level in plan.narrow:
         onehot[pl.ds(plan.offsets[level], kinds * plan.padded[level]), :] = narrow_onehot(
             plan, pattern_ref[...], level, 0)
+    turned = pattern_ref[...].T
+    for level in plan.narrow:
+        columns = pl.ds(plan.offsets[level], kinds * plan.padded[level])
+        spread_ref[:, columns] = narrow_onehot(plan, turned, level, 1)
+    spread_ref[:, pl.ds(plan.narrow_rows, plan.wide_rows)] = wide_rows_onehot(plan, turned, 1)
+    before[:, pl.ds(0, 8), :] = jnp.zeros((2, 8, width), F32)
+    after[:, pl.ds(blocks, 8), :] = jnp.zeros((2, 8, width), F32)
+    for copy in weight_copies[1:]:
+        copy.wait()
 
     def narrow(step, _):
         here = chunk_of(step)
+        stencils = jnp.concatenate([stencil_ref[0], stencil_ref[1], stencil_ref[2]], axis=1)
         for first in range(0, chunk, 2):
             at = step * chunk + first
             both = jnp.concatenate([fine_ref[at], fine_ref[at + 1]], axis=1)
             both = jnp.dot(onehot[...], both, preferred_element_type=F32).astype(BF16)
             grouped[first] = both[:, :width]
             grouped[first + 1] = both[:, width:]
+        for slot in range(chunk):
+            at = step * chunk + slot
+            three = jnp.dot(fine_ref[at], stencils, preferred_element_type=F32)
+            turn = slot % 2
+            before[turn, pl.ds(8, blocks), :] = three[:, :width]
+            after[turn, pl.ds(0, blocks), :] = three[:, 2 * width :]
+            level0_ref[at] = (three[:, width : 2 * width] + before[turn, pl.ds(7, blocks), :]
+                              + after[turn, pl.ds(1, blocks), :])
         for level in plan.narrow:
             padded = plan.padded[level]
             slices = [pl.ds(plan.offsets[level] + kind * padded, padded) for kind in range(kinds)]
@@ -190,8 +216,7 @@
             lifted = lax.dot_general(
                 solved, restrict_ref[level], (((1,), (1,)), ((), ())), preferred_element_type=F32).astype(BF16)
             for kind, tile in enumerate(slices):
-                lifted_ref[here, tile, :] = lifted[:, kind * width : (kind + 1) * width].reshape(chunk, padded, width)
-        lifted_copy(step).start()
+                table_ref[here, tile, :] = lifted[:, kind * width : (kind + 1) * width].reshape(chunk, padded, width)
         return 0
 
     def lift_wide(position, rounded):
@@ -203,7 +228,7 @@
             wide_f32[:, position * kinds + kind, :] = lifted[:, kind * width : (kind + 1) * width]
 
     first_stop = steps // 4
-    second_stop = steps - max(steps // 4, 1)
+    second_stop = steps // 2
     lax.fori_loop(0, first_stop, narrow, 0)
 
     total = coarse_ref[pl.ds(local, crossing), part_of(mine), :].astype(F32)
@@ -221,8 +246,12 @@
     for copy in column_copies:
         copy.start()
 
+    for copy in halo_copies:
+        copy.wait_recv()
     for row in range(plan.wide_used, plan.wide_rows):
         wide_f32[:, row, :] = jnp.zeros((plan.vectors, width), F32)
+    wide_f32[:, base, :] = jnp.dot(beside_ref[0], stencil_ref[0], preferred_element_type=F32)
+    wide_f32[:, base + 1, :] = jnp.dot(beside_ref[1], stencil_ref[2], preferred_element_type=F32)
     for position in range(local):
         lift_wide(position, coarse_ref[position])
     lax.fori_loop(first_stop, second_stop, narrow, 0)
@@ -249,8 +278,6 @@
         copy.start()
 
     lax.fori_loop(second_stop, steps, narrow, 0)
-    for copy in halo_copies:
-        copy.wait_recv()
     for copy in copies:
         copy.wait_send()
     coarse_ref[pl.ds(local, crossing), part_of(mine), :] = to_group[...]
@@ -260,49 +287,27 @@
         coarse_ref[pl.ds(local, crossing), part_of(source), :] = back[apart]
     for position in range(local, len(plan.wide)):
         lift_wide(position, coarse_ref[position])
-    wide_ref[...] = wide_f32[...].astype(BF16)
-    wide_copy = pltpu.make_async_copy(wide_ref, wide_hbm, wide_sem)
-    wide_copy.start()
-    for step in range(steps):
-        lifted_copy(step).wait()
+    table_ref[:, pl.ds(plan.narrow_rows, plan.wide_rows), :] = wide_f32[:, pl.ds(0, plan.wide_rows), :].astype(BF16)
     for copy in halo_copies + column_copies + back_copies:
         copy.wait_send()
-    wide_copy.wait()
-
-
-def final_kernel(plan, chunk, pattern_ref, beside_ref, stencil_ref,
-                 fine_ref, lifted_ref, wide_ref, out_ref, spread, halo, before, after):
-    step = pl.program_id(0)
-    width, blocks = plan.width, plan.blocks
-
-    @pl.when(step == 0)
-    def _():
-        turned = pattern_ref[...].T
-        for level in plan.narrow:
-            columns = pl.ds(plan.offsets[level], plan.kinds * plan.padded[level])
-            spread[:, columns] = narrow_onehot(plan, turned, level, 1)
-        spread[:, pl.ds(plan.narrow_rows, plan.wide_rows)] = wide_rows_onehot(plan, turned, 1)
-        halo[0] = jnp.dot(beside_ref[0], stencil_ref[0], preferred_element_type=F32)
-        halo[1] = jnp.dot(beside_ref[1], stencil_ref[2], preferred_element_type=F32)
-
-    stencils = jnp.concatenate([stencil_ref[0], stencil_ref[1], stencil_ref[2]], axis=1)
-    for first in range(0, chunk, 2):
-        tables = [jnp.concatenate([lifted_ref[first + slot], wide_ref[first + slot]], axis=0) for slot in range(2)]
-        both = jnp.dot(spread[...], jnp.concatenate(tables, axis=1), preferred_element_type=F32)
-        for slot in range(2):
-            vector = pl.ds(step * chunk + first + slot, 1)
-            three = jnp.dot(fine_ref[first + slot], stencils, preferred_element_type=F32)
-            before[slot, pl.ds(7, 1), :] = halo[0, vector, :]
-            before[slot, pl.ds(8, blocks), :] = three[:, :width]
-            after[slot, pl.ds(0, blocks), :] = three[:, 2 * width :]
-            after[slot, pl.ds(blocks, 1), :] = halo[1, vector, :]
-            result = both[:, slot * width : (slot + 1) * width] + three[:, width : 2 * width]
-            result = result + before[slot, pl.ds(7, blocks), :]
-            out_ref[first + slot] = result + after[slot, pl.ds(1, blocks), :]
-
-
-def whole(ndim_shape):
-    return pl.BlockSpec(ndim_shape, lambda *_: (0,) * len(ndim_shape))
+
+
+def final_kernel(plan, pieces, spread_ref, table_ref, level0_ref, out_hbm, staged, out_sem):
+    width = plan.width
+    copies, at = [], 0
+    for index, piece in enumerate(pieces):
+        for first in range(at, at + piece, 2):
+            tables = jnp.concatenate([table_ref[first], table_ref[first + 1]], axis=1)
+            both = jnp.dot(spread_ref[...], tables, preferred_element_type=F32)
+            staged[first] = both[:, :width] + level0_ref[first]
+            staged[first + 1] = both[:, width:] + level0_ref[first + 1]
+        here = pl.ds(at, piece)
+        copy = pltpu.make_async_copy(staged.at[here], out_hbm.at[here], out_sem.at[index])
+        copy.start()
+        copies.append(copy)
+        at += piece
+    for copy in copies:
+        copy.wait()
 
 
 def shards(fine, pattern, stencil, restrict, coarse_inv):
@@ -312,73 +317,65 @@
     plan = Plan(devices, vectors, blocks, width, levels, kinds)
     stacked = restrict.reshape(levels, kinds * width, width)
     wide_count = len(plan.wide)
-    params = pltpu.CompilerParams(dimension_semantics=("arbitrary",), vmem_limit_bytes=VMEM_LIMIT)
-    chunk = 16
-    steps = vectors // chunk
+    chunk = 8
     near = plan.groups[plan.crossing[0]]
     far = devices // near
     crossing = len(plan.crossing)
     part = vectors // near
+    table_rows = plan.narrow_rows + plan.wide_rows
     vmem = pl.BlockSpec(memory_space=pltpu.VMEM)
-    hbm = pl.BlockSpec(memory_space=pl.ANY)
+    hbm = pl.BlockSpec(memory_space=pltpu.HBM)
     dma = pltpu.SemaphoreType.DMA
-    lifted, wide, beside = pl.pallas_call(
+    pinned = [pltpu.with_memory_space_constraint(x, pltpu.HBM) for x in (pattern, fine, stacked, coarse_inv, stencil)]
+    table, level0, spread = pl.pallas_call(
         functools.partial(exchange_kernel, plan, chunk),
         out_shape=(
-            jax.ShapeDtypeStruct((vectors, plan.narrow_rows, width), BF16),
-            jax.ShapeDtypeStruct((vectors, plan.wide_rows, width), BF16),
-            jax.ShapeDtypeStruct((2, vectors, width), BF16),
+            pltpu.VMEM((vectors, table_rows, width), BF16),
+            pltpu.VMEM((vectors, blocks, width), F32),
+            pltpu.VMEM((blocks, table_rows), BF16),
         ),
-        in_specs=[vmem, hbm, hbm, hbm],
-        out_specs=(hbm, hbm, vmem),
+        in_specs=[hbm] * 5,
+        out_specs=(vmem, vmem, vmem),
         scratch_shapes=[
+            pltpu.VMEM(pattern.shape, jnp.int32),
             pltpu.VMEM(fine.shape, BF16),
             pltpu.VMEM(stacked.shape, BF16),
             pltpu.VMEM(coarse_inv.shape, BF16),
-            pltpu.VMEM((vectors, plan.narrow_rows, width), BF16),
-            pltpu.VMEM((vectors, plan.wide_rows, width), BF16),
-            pltpu.VMEM((vectors, plan.wide_rows, width), F32),
+            pltpu.VMEM(stencil.shape, BF16),
+            pltpu.VMEM((vectors, PITCH, width), F32),
             pltpu.VMEM((plan.wide_rows, blocks), BF16),
             pltpu.VMEM((plan.narrow_rows, blocks), BF16),
-            pltpu.VMEM((chunk, plan.wide_rows, width), F32),
+            pltpu.VMEM((16, PITCH, width), F32),
             pltpu.VMEM((chunk, plan.narrow_rows, width), BF16),
             pltpu.VMEM((plan.wide_used, vectors, width), BF16),
             pltpu.VMEM((wide_count, vectors, width), BF16),
             pltpu.VMEM((2, vectors, width), BF16),
+            pltpu.VMEM((2, vectors, width), BF16),
+            pltpu.VMEM((2, blocks + 8, width), F32),
+            pltpu.VMEM((2, blocks + 8, width), F32),
             pltpu.VMEM((near, crossing, part, width), BF16),
             pltpu.VMEM((crossing, part, width), BF16),
             pltpu.VMEM((far, crossing - 1, part, width), BF16),
             pltpu.VMEM((crossing, part, width), BF16),
             pltpu.VMEM((near, crossing, part, width), BF16),
-            dma((steps,)), dma((2,)), dma((steps,)), dma,
+            dma((vectors // 16,)), dma((5,)),
             dma((near,)), dma((near,)), dma((far,)), dma((far,)), dma((near,)), dma((near,)), dma((2,)), dma((2,)),
         ],
         compiler_params=pltpu.CompilerParams(
             collective_id=0, has_side_effects=True, vmem_limit_bytes=VMEM_LIMIT),
         name="exchange",
-    )(pattern, fine, stacked, coarse_inv)
-
-    last = 8
+    )(*pinned)
+
+    pieces = [8] * (vectors // 8 - 1) + [4, 2, 2]
     return pl.pallas_call(
-        functools.partial(final_kernel, plan, last),
-        grid=(vectors // last,),
+        functools.partial(final_kernel, plan, pieces),
         out_shape=jax.ShapeDtypeStruct(fine.shape, F32),
-        in_specs=[
-            whole(pattern.shape), whole(beside.shape), whole(stencil.shape),
-            pl.BlockSpec((last, blocks, width), lambda i: (i, 0, 0)),
-            pl.BlockSpec((last, plan.narrow_rows, width), lambda i: (i, 0, 0)),
-            pl.BlockSpec((last, plan.wide_rows, width), lambda i: (i, 0, 0)),
-        ],
-        out_specs=pl.BlockSpec((last, blocks, width), lambda i: (i, 0, 0)),
-        scratch_shapes=[
-            pltpu.VMEM((blocks, plan.narrow_rows + plan.wide_rows), BF16),
-            pltpu.VMEM((2, vectors, width), F32),
-            pltpu.VMEM((2, blocks + 8, width), F32),
-            pltpu.VMEM((2, blocks + 8, width), F32),
-        ],
-        compiler_params=params,
+        in_specs=[vmem, vmem, vmem],
+        out_specs=pl.BlockSpec(memory_space=pl.ANY),
+        scratch_shapes=[pltpu.VMEM(fine.shape, F32), dma((len(pieces),))],
+        compiler_params=pltpu.CompilerParams(vmem_limit_bytes=VMEM_LIMIT),
         name="final",
-    )(pattern, beside, stencil, fine, lifted, wide)
+    )(spread, table, level0)
 
 
 def solution(mesh):

time: 33.9 us -> 28.7 us (0.85)
  Pallas kernels: 33.5 us -> 28.5 us
    pallas_call x1, Pallas kernels: 13.2 us -> 3.79 us  [shards(): pl.pallas_call(functools.partial(final_kernel, plan, pieces), out_shape=j...]
    pallas_call x1, Pallas kernels: 20.3 us -> 24.7 us  [shards(): pl.pallas_call(functools.partial(exchange_kernel, plan, chunk), out_shape...]
where the time goes in v1:
time: 28.7 us; the launch traced here: 28.5 us
  Pallas kernels  28.5 us (99%)
    pallas_call x1, Pallas kernels, shards(): pl.pallas_call(functools.partial(exchange_kernel, plan, chunk), out_shape...  24.7 us
    pallas_call x1, Pallas kernels, shards(): pl.pallas_call(functools.partial(final_kernel, plan, pieces), out_shape=j...  3.79 us

profile of v1, /device:TPU:0, one launch (start us, length us, event | category | flops | bytes accessed | tf_op | source)
XLA Modules:
  0.0 28.5 jit_solution(9715239591482858918)
XLA Ops:
  0.0 24.7 %exchange.1 = (bf16[64,416,128]{2,1,0:T(8,128)(2,1)S(1)}, f32[64,256,128]{2,1,0:T(8,128)S(1)}, bf16[256,416]{1,0:T(8,128)(2,1)S(1)}) custom-call(s32[8,256]{1,0:T(8,128)} %pattern_hbm.1, bf16[64,256,128]{2,1,0:T(8,128)(2,1)} %fine_hbm.1, bf16[8,512,128]{2,1,0:T(8,128)(2,1)} %bitcast.1, bf16[8,128,128]{2,1,0:T(8,128)(2,1)} %inverse_hbm.1, ...), custom_call_target="tpu_custom_call" | custom-call | tf_op jit(solution)/shard_map/exchange/pallas_call | solution.py:330
  24.7 3.8 %final.1 = f32[64,256,128]{2,1,0:T(8,128)} custom-call(bf16[256,416]{1,0:T(8,128)(2,1)S(1)} %get-tuple-element.8.spread_ref, bf16[64,416,128]{2,1,0:T(8,128)(2,1)S(1)} %get-tuple-element.9.table_ref, f32[64,256,128]{2,1,0:T(8,128)S(1)} %get-tuple-element.10.level0_ref), custom_call_target="tpu_custom_call" | custom-call | tf_op jit(solution)/shard_map/final/pallas_call | solution.py:370

commit v2 on v1

--- a/solution.py
+++ b/solution.py
@@ -74,7 +74,7 @@
 def exchange_kernel(plan, chunk, pattern_hbm, fine_hbm, restrict_hbm, inverse_hbm, stencil_hbm,
                     table_ref, level0_ref, spread_ref,
                     pattern_ref, fine_ref, restrict_ref, inverse_ref, stencil_ref, wide_f32, wide_onehot, onehot, few,
-                    grouped, rows, coarse_ref, halo_ref, beside_ref, before, after,
+                    grouped, joint, rows, coarse_ref, halo_ref, beside_ref,
                     from_group, to_column, from_column, to_group, back,
                     fine_sem, weight_sem, group_send, group_recv,
                     column_send, column_recv, back_send, back_recv, halo_send, halo_recv):
@@ -131,18 +131,30 @@
 
     pattern_copy.wait()
     wide_onehot[...] = wide_rows_onehot(plan, pattern_ref[...], 0)
+    for level in plan.narrow:
+        onehot[pl.ds(plan.offsets[level], kinds * plan.padded[level]), :] = narrow_onehot(
+            plan, pattern_ref[...], level, 0)
+    turned = pattern_ref[...].T
+    for level in plan.narrow:
+        columns = pl.ds(plan.offsets[level], kinds * plan.padded[level])
+        spread_ref[:, columns] = narrow_onehot(plan, turned, level, 1)
+    spread_ref[:, pl.ds(plan.narrow_rows, plan.wide_rows)] = wide_rows_onehot(plan, turned, 1)
+
+    def extract(step):
+        for row in range(plan.wide_used):
+            rows[row, pl.ds(step * load, load), :] = few[step % 2, pl.ds(row, load, stride=PITCH), :].astype(BF16)
 
     for step in range(loads):
         fine_copy(step).wait()
-        here = pl.ds(step * load, load)
         for first in range(0, load, 2):
             at = step * load + first
             both = jnp.concatenate([fine_ref[at], fine_ref[at + 1]], axis=1)
             both = jnp.dot(wide_onehot[...], both, preferred_element_type=F32)
-            few[first, pl.ds(0, plan.wide_rows), :] = both[:, :width]
-            few[first + 1, pl.ds(0, plan.wide_rows), :] = both[:, width:]
-        for row in range(plan.wide_used):
-            rows[row, here, :] = few[:, row, :].astype(BF16)
+            few[step % 2, pl.ds(first * PITCH, plan.wide_rows), :] = both[:, :width]
+            few[step % 2, pl.ds((first + 1) * PITCH, plan.wide_rows), :] = both[:, width:]
+        if step > 0:
+            extract(step - 1)
+    extract(loads - 1)
     weight_copies[0].wait()
     for position, level in enumerate(plan.wide):
         first = position * kinds
@@ -175,18 +187,14 @@
     for copy in copies + halo_copies:
         copy.start()
 
-    for level in plan.narrow:
-        onehot[pl.ds(plan.offsets[level], kinds * plan.padded[level]), :] = narrow_onehot(
-            plan, pattern_ref[...], level, 0)
-    turned = pattern_ref[...].T
-    for level in plan.narrow:
-        columns = pl.ds(plan.offsets[level], kinds * plan.padded[level])
-        spread_ref[:, columns] = narrow_onehot(plan, turned, level, 1)
-    spread_ref[:, pl.ds(plan.narrow_rows, plan.wide_rows)] = wide_rows_onehot(plan, turned, 1)
-    before[:, pl.ds(0, 8), :] = jnp.zeros((2, 8, width), F32)
-    after[:, pl.ds(blocks, 8), :] = jnp.zeros((2, 8, width), F32)
     for copy in weight_copies[1:]:
         copy.wait()
+    for position, level in enumerate(plan.narrow):
+        half = jnp.dot(restrict_ref[level], inverse_ref[level], preferred_element_type=F32).astype(BF16)
+        full = lax.dot_general(half, restrict_ref[level], (((1,), (1,)), ((), ())), preferred_element_type=F32)
+        joint[position] = (full * plan.spans[level] ** (-0.5)).astype(BF16)
+
+    edge = lax.broadcasted_iota(jnp.int32, (blocks, width), 0)
 
     def narrow(step, _):
         here = chunk_of(step)
@@ -200,21 +208,15 @@
         for slot in range(chunk):
             at = step * chunk + slot
             three = jnp.dot(fine_ref[at], stencils, preferred_element_type=F32)
-            turn = slot % 2
-            before[turn, pl.ds(8, blocks), :] = three[:, :width]
-            after[turn, pl.ds(0, blocks), :] = three[:, 2 * width :]
-            level0_ref[at] = (three[:, width : 2 * width] + before[turn, pl.ds(7, blocks), :]
-                              + after[turn, pl.ds(1, blocks), :])
-        for level in plan.narrow:
+            earlier = jnp.where(edge == 0, 0.0, pltpu.roll(three[:, :width], 1, 0))
+            later = jnp.where(edge == blocks - 1, 0.0, pltpu.roll(three[:, 2 * width :], blocks - 1, 0))
+            level0_ref[at] = three[:, width : 2 * width] + earlier + later
+        for position, level in enumerate(plan.narrow):
             padded = plan.padded[level]
             slices = [pl.ds(plan.offsets[level] + kind * padded, padded) for kind in range(kinds)]
             joined = jnp.concatenate(
                 [grouped[:, tile, :].reshape(chunk * padded, width) for tile in slices], axis=1)
-            coarse = jnp.dot(joined, restrict_ref[level], preferred_element_type=F32)
-            rounded = (coarse * plan.spans[level] ** (-0.5)).astype(BF16)
-            solved = jnp.dot(rounded, inverse_ref[level], preferred_element_type=F32).astype(BF16)
-            lifted = lax.dot_general(
-                solved, restrict_ref[level], (((1,), (1,)), ((), ())), preferred_element_type=F32).astype(BF16)
+            lifted = jnp.dot(joined, joint[position], preferred_element_type=F32).astype(BF16)
             for kind, tile in enumerate(slices):
                 table_ref[here, tile, :] = lifted[:, kind * width : (kind + 1) * width].reshape(chunk, padded, width)
         return 0
@@ -225,7 +227,8 @@
         lifted = lax.dot_general(
             solved, restrict_ref[level], (((1,), (1,)), ((), ())), preferred_element_type=F32)
         for kind in range(kinds):
-            wide_f32[:, position * kinds + kind, :] = lifted[:, kind * width : (kind + 1) * width]
+            wide_f32[pl.ds(position * kinds + kind, plan.vectors, stride=PITCH), :] = (
+                lifted[:, kind * width : (kind + 1) * width])
 
     first_stop = steps // 4
     second_stop = steps // 2
@@ -249,9 +252,9 @@
     for copy in halo_copies:
         copy.wait_recv()
     for row in range(plan.wide_used, plan.wide_rows):
-        wide_f32[:, row, :] = jnp.zeros((plan.vectors, width), F32)
-    wide_f32[:, base, :] = jnp.dot(beside_ref[0], stencil_ref[0], preferred_element_type=F32)
-    wide_f32[:, base + 1, :] = jnp.dot(beside_ref[1], stencil_ref[2], preferred_element_type=F32)
+        wide_f32[pl.ds(row, plan.vectors, stride=PITCH), :] = jnp.zeros((plan.vectors, width), F32)
+    wide_f32[pl.ds(base, plan.vectors, stride=PITCH), :] = jnp.dot(beside_ref[0], stencil_ref[0], preferred_element_type=F32)
+    wide_f32[pl.ds(base + 1, plan.vectors, stride=PITCH), :] = jnp.dot(beside_ref[1], stencil_ref[2], preferred_element_type=F32)
     for position in range(local):
         lift_wide(position, coarse_ref[position])
     lax.fori_loop(first_stop, second_stop, narrow, 0)
@@ -287,7 +290,9 @@
         coarse_ref[pl.ds(local, crossing), part_of(source), :] = back[apart]
     for position in range(local, len(plan.wide)):
         lift_wide(position, coarse_ref[position])
-    table_ref[:, pl.ds(plan.narrow_rows, plan.wide_rows), :] = wide_f32[:, pl.ds(0, plan.wide_rows), :].astype(BF16)
+    for vector in range(plan.vectors):
+        table_ref[vector, pl.ds(plan.narrow_rows, plan.wide_rows), :] = (
+            wide_f32[pl.ds(vector * PITCH, plan.wide_rows), :].astype(BF16))
     for copy in halo_copies + column_copies + back_copies:
         copy.wait_send()
 
@@ -317,7 +322,7 @@
     plan = Plan(devices, vectors, blocks, width, levels, kinds)
     stacked = restrict.reshape(levels, kinds * width, width)
     wide_count = len(plan.wide)
-    chunk = 8
+    chunk = 16
     near = plan.groups[plan.crossing[0]]
     far = devices // near
     crossing = len(plan.crossing)
@@ -342,17 +347,16 @@
             pltpu.VMEM(stacked.shape, BF16),
             pltpu.VMEM(coarse_inv.shape, BF16),
             pltpu.VMEM(stencil.shape, BF16),
-            pltpu.VMEM((vectors, PITCH, width), F32),
+            pltpu.VMEM((vectors * PITCH, width), F32),
             pltpu.VMEM((plan.wide_rows, blocks), BF16),
             pltpu.VMEM((plan.narrow_rows, blocks), BF16),
-            pltpu.VMEM((16, PITCH, width), F32),
+            pltpu.VMEM((2, 16 * PITCH, width), F32),
             pltpu.VMEM((chunk, plan.narrow_rows, width), BF16),
+            pltpu.VMEM((len(plan.narrow), kinds * width, kinds * width), BF16),
             pltpu.VMEM((plan.wide_used, vectors, width), BF16),
             pltpu.VMEM((wide_count, vectors, width), BF16),
             pltpu.VMEM((2, vectors, width), BF16),
             pltpu.VMEM((2, vectors, width), BF16),
-            pltpu.VMEM((2, blocks + 8, width), F32),
-            pltpu.VMEM((2, blocks + 8, width), F32),
             pltpu.VMEM((near, crossing, part, width), BF16),
             pltpu.VMEM((crossing, part, width), BF16),
             pltpu.VMEM((far, crossing - 1, part, width), BF16),

time: 28.7 us -> 23.9 us (0.83)
  Pallas kernels: 28.5 us -> 23.7 us
    pallas_call x1, Pallas kernels: 24.7 us -> 19.9 us  [shards(): pl.pallas_call(functools.partial(exchange_kernel, plan, chunk), out_shape...]
where the time goes in v2:
time: 23.9 us; the launch traced here: 23.7 us
  Pallas kernels  23.7 us (99%)
    pallas_call x1, Pallas kernels, shards(): pl.pallas_call(functools.partial(exchange_kernel, plan, chunk), out_shape...  19.9 us
    pallas_call x1, Pallas kernels, shards(): pl.pallas_call(functools.partial(final_kernel, plan, pieces), out_shape=j...  3.79 us

profile of v2, /device:TPU:0, one launch (start us, length us, event | category | flops | bytes accessed | tf_op | source)
XLA Modules:
  0.0 23.7 jit_solution(10273935557737319641)
XLA Ops:
  0.0 19.9 %exchange.1 = (bf16[64,416,128]{2,1,0:T(8,128)(2,1)S(1)}, f32[64,256,128]{2,1,0:T(8,128)S(1)}, bf16[256,416]{1,0:T(8,128)(2,1)S(1)}) custom-call(s32[8,256]{1,0:T(8,128)} %pattern_hbm.1, bf16[64,256,128]{2,1,0:T(8,128)(2,1)} %fine_hbm.1, bf16[8,512,128]{2,1,0:T(8,128)(2,1)} %bitcast.1, bf16[8,128,128]{2,1,0:T(8,128)(2,1)} %inverse_hbm.1, ...), custom_call_target="tpu_custom_call" | custom-call | tf_op jit(solution)/shard_map/exchange/pallas_call | solution.py:335
  19.9 3.8 %final.1 = f32[64,256,128]{2,1,0:T(8,128)} custom-call(bf16[256,416]{1,0:T(8,128)(2,1)S(1)} %get-tuple-element.8.spread_ref, bf16[64,416,128]{2,1,0:T(8,128)(2,1)S(1)} %get-tuple-element.9.table_ref, f32[64,256,128]{2,1,0:T(8,128)S(1)} %get-tuple-element.10.level0_ref), custom_call_target="tpu_custom_call" | custom-call | tf_op jit(solution)/shard_map/final/pallas_call | solution.py:374

commit v3 on v2

--- a/solution.py
+++ b/solution.py
@@ -71,17 +71,16 @@
 PITCH = 40
 
 
-def exchange_kernel(plan, chunk, pattern_hbm, fine_hbm, restrict_hbm, inverse_hbm, stencil_hbm,
+def exchange_kernel(plan, segments, pattern_hbm, fine_hbm, restrict_hbm, inverse_hbm, stencil_hbm,
                     table_ref, level0_ref, spread_ref,
                     pattern_ref, fine_ref, restrict_ref, inverse_ref, stencil_ref, wide_f32, wide_onehot, onehot, few,
-                    grouped, joint, rows, coarse_ref, halo_ref, beside_ref,
+                    grouped, joint, pair_weights, split, rows, coarse_ref, halo_ref, beside_ref,
                     from_group, to_column, from_column, to_group, back,
                     fine_sem, weight_sem, group_send, group_recv,
                     column_send, column_recv, back_send, back_recv, halo_send, halo_recv):
     width, kinds, blocks = plan.width, plan.kinds, plan.blocks
     load = 16
     loads = plan.vectors // load
-    steps = plan.vectors // chunk
     devices = plan.devices
     near = plan.groups[plan.crossing[0]]
     far = devices // near
@@ -91,9 +90,6 @@
     me = lax.axis_index("gx")
     mine = lax.rem(me, near)
     place = me // near
-
-    def chunk_of(step):
-        return pl.ds(pl.multiple_of(step * chunk, chunk), chunk)
 
     def fine_copy(step):
         here = pl.ds(step * load, load)
@@ -194,32 +190,42 @@
         full = lax.dot_general(half, restrict_ref[level], (((1,), (1,)), ((), ())), preferred_element_type=F32)
         joint[position] = (full * plan.spans[level] ** (-0.5)).astype(BF16)
 
-    edge = lax.broadcasted_iota(jnp.int32, (blocks, width), 0)
-
-    def narrow(step, _):
-        here = chunk_of(step)
-        stencils = jnp.concatenate([stencil_ref[0], stencil_ref[1], stencil_ref[2]], axis=1)
-        for first in range(0, chunk, 2):
-            at = step * chunk + first
+    none = jnp.zeros((width, width), BF16)
+    pair_weights[...] = jnp.concatenate([
+        jnp.concatenate([stencil_ref[1], stencil_ref[0], none, stencil_ref[2]], axis=1),
+        jnp.concatenate([stencil_ref[2], stencil_ref[1], stencil_ref[0], none], axis=1)], axis=0)
+    pairs = blocks // 2
+    edge = lax.broadcasted_iota(jnp.int32, (pairs, width), 0)
+    ahead = (edge > 0).astype(F32)
+    behind = (edge < pairs - 1).astype(F32)
+
+    def narrow(start, chunk):
+        for slot in range(0, chunk, 2):
+            at = start + slot
             both = jnp.concatenate([fine_ref[at], fine_ref[at + 1]], axis=1)
             both = jnp.dot(onehot[...], both, preferred_element_type=F32).astype(BF16)
-            grouped[first] = both[:, :width]
-            grouped[first + 1] = both[:, width:]
+            grouped[slot] = both[:, :width]
+            grouped[slot + 1] = both[:, width:]
         for slot in range(chunk):
-            at = step * chunk + slot
-            three = jnp.dot(fine_ref[at], stencils, preferred_element_type=F32)
-            earlier = jnp.where(edge == 0, 0.0, pltpu.roll(three[:, :width], 1, 0))
-            later = jnp.where(edge == blocks - 1, 0.0, pltpu.roll(three[:, 2 * width :], blocks - 1, 0))
-            level0_ref[at] = three[:, width : 2 * width] + earlier + later
+            at = start + slot
+            turn = slot % 4
+            split[turn] = fine_ref[at].astype(F32)
+            evens = split[turn, pl.ds(0, pairs, stride=2), :].astype(BF16)
+            odds = split[turn, pl.ds(1, pairs, stride=2), :].astype(BF16)
+            four = jnp.dot(jnp.concatenate([evens, odds], axis=1), pair_weights[...], preferred_element_type=F32)
+            earlier = pltpu.roll(four[:, 2 * width : 3 * width], 1, 0) * ahead
+            later = pltpu.roll(four[:, 3 * width :], pairs - 1, 0) * behind
+            level0_ref[at, pl.ds(0, pairs, stride=2), :] = four[:, :width] + earlier
+            level0_ref[at, pl.ds(1, pairs, stride=2), :] = four[:, width : 2 * width] + later
         for position, level in enumerate(plan.narrow):
             padded = plan.padded[level]
             slices = [pl.ds(plan.offsets[level] + kind * padded, padded) for kind in range(kinds)]
             joined = jnp.concatenate(
-                [grouped[:, tile, :].reshape(chunk * padded, width) for tile in slices], axis=1)
+                [grouped[pl.ds(0, chunk), tile, :].reshape(chunk * padded, width) for tile in slices], axis=1)
             lifted = jnp.dot(joined, joint[position], preferred_element_type=F32).astype(BF16)
             for kind, tile in enumerate(slices):
-                table_ref[here, tile, :] = lifted[:, kind * width : (kind + 1) * width].reshape(chunk, padded, width)
-        return 0
+                table_ref[pl.ds(start, chunk), tile, :] = (
+                    lifted[:, kind * width : (kind + 1) * width].reshape(chunk, padded, width))
 
     def lift_wide(position, rounded):
         level = plan.wide[position]
@@ -230,9 +236,8 @@
             wide_f32[pl.ds(position * kinds + kind, plan.vectors, stride=PITCH), :] = (
                 lifted[:, kind * width : (kind + 1) * width])
 
-    first_stop = steps // 4
-    second_stop = steps // 2
-    lax.fori_loop(0, first_stop, narrow, 0)
+    starts = [sum(segments[:index]) for index in range(len(segments))]
+    narrow(starts[0], segments[0])
 
     total = coarse_ref[pl.ds(local, crossing), part_of(mine), :].astype(F32)
     for apart, copy in enumerate(copies, 1):
@@ -257,7 +262,7 @@
     wide_f32[pl.ds(base + 1, plan.vectors, stride=PITCH), :] = jnp.dot(beside_ref[1], stencil_ref[2], preferred_element_type=F32)
     for position in range(local):
         lift_wide(position, coarse_ref[position])
-    lax.fori_loop(first_stop, second_stop, narrow, 0)
+    narrow(starts[1], segments[1])
 
     to_group[0] = to_column[0]
     sums = [to_column[index].astype(F32) for index in range(crossing)]
@@ -280,7 +285,7 @@
     for copy in back_copies:
         copy.start()
 
-    lax.fori_loop(second_stop, steps, narrow, 0)
+    narrow(starts[2], segments[2])
     for copy in copies:
         copy.wait_send()
     coarse_ref[pl.ds(local, crossing), part_of(mine), :] = to_group[...]
@@ -322,7 +327,8 @@
     plan = Plan(devices, vectors, blocks, width, levels, kinds)
     stacked = restrict.reshape(levels, kinds * width, width)
     wide_count = len(plan.wide)
-    chunk = 16
+    some = vectors // 4
+    segments = (some, 2 * some, vectors - 3 * some)
     near = plan.groups[plan.crossing[0]]
     far = devices // near
     crossing = len(plan.crossing)
@@ -333,7 +339,7 @@
     dma = pltpu.SemaphoreType.DMA
     pinned = [pltpu.with_memory_space_constraint(x, pltpu.HBM) for x in (pattern, fine, stacked, coarse_inv, stencil)]
     table, level0, spread = pl.pallas_call(
-        functools.partial(exchange_kernel, plan, chunk),
+        functools.partial(exchange_kernel, plan, segments),
         out_shape=(
             pltpu.VMEM((vectors, table_rows, width), BF16),
             pltpu.VMEM((vectors, blocks, width), F32),
@@ -351,8 +357,10 @@
             pltpu.VMEM((plan.wide_rows, blocks), BF16),
             pltpu.VMEM((plan.narrow_rows, blocks), BF16),
             pltpu.VMEM((2, 16 * PITCH, width), F32),
-            pltpu.VMEM((chunk, plan.narrow_rows, width), BF16),
+            pltpu.VMEM((max(segments), plan.narrow_rows, width), BF16),
             pltpu.VMEM((len(plan.narrow), kinds * width, kinds * width), BF16),
+            pltpu.VMEM((2 * width, 4 * width), BF16),
+            pltpu.VMEM((4, blocks, width), F32),
             pltpu.VMEM((plan.wide_used, vectors, width), BF16),
             pltpu.VMEM((wide_count, vectors, width), BF16),
             pltpu.VMEM((2, vectors, width), BF16),
@@ -370,7 +378,7 @@
         name="exchange",
     )(*pinned)
 
-    pieces = [8] * (vectors // 8 - 1) + [4, 2, 2]
+    pieces = [2, 2, 4] + [8] * (vectors // 8 - 2) + [4, 2, 2]
     return pl.pallas_call(
         functools.partial(final_kernel, plan, pieces),
         out_shape=jax.ShapeDtypeStruct(fine.shape, F32),

time: 23.9 us -> 22.2 us (0.929)
  Pallas kernels: 23.7 us -> 22 us
    pallas_call x1, Pallas kernels: 19.9 us -> 18.2 us  [shards(): pl.pallas_call(functools.partial(exchange_kernel, plan, segments), out_sh...]
where the time goes in v3:
time: 22.2 us; the launch traced here: 22 us
  Pallas kernels  22 us (99%)
    pallas_call x1, Pallas kernels, shards(): pl.pallas_call(functools.partial(exchange_kernel, plan, segments), out_sh...  18.2 us
    pallas_call x1, Pallas kernels, shards(): pl.pallas_call(functools.partial(final_kernel, plan, pieces), out_shape=j...  3.77 us

profile of v3, /device:TPU:0, one launch (start us, length us, event | category | flops | bytes accessed | tf_op | source)
XLA Modules:
  0.0 22.0 jit_solution(1914616790945324335)
XLA Ops:
  0.0 18.2 %exchange.1 = (bf16[64,416,128]{2,1,0:T(8,128)(2,1)S(1)}, f32[64,256,128]{2,1,0:T(8,128)S(1)}, bf16[256,416]{1,0:T(8,128)(2,1)S(1)}) custom-call(s32[8,256]{1,0:T(8,128)} %pattern_hbm.1, bf16[64,256,128]{2,1,0:T(8,128)(2,1)} %fine_hbm.1, bf16[8,512,128]{2,1,0:T(8,128)(2,1)} %bitcast.1, bf16[8,128,128]{2,1,0:T(8,128)(2,1)} %inverse_hbm.1, ...), custom_call_target="tpu_custom_call" | custom-call | tf_op jit(solution)/shard_map/exchange/pallas_call | solution.py:341
  18.3 3.8 %final.1 = f32[64,256,128]{2,1,0:T(8,128)} custom-call(bf16[256,416]{1,0:T(8,128)(2,1)S(1)} %get-tuple-element.8.spread_ref, bf16[64,416,128]{2,1,0:T(8,128)(2,1)S(1)} %get-tuple-element.9.table_ref, f32[64,256,128]{2,1,0:T(8,128)S(1)} %get-tuple-element.10.level0_ref), custom_call_target="tpu_custom_call" | custom-call | tf_op jit(solution)/shard_map/final/pallas_call | solution.py:382

commit v4 on v3

--- a/solution.py
+++ b/solution.py
@@ -34,12 +34,15 @@
         self.narrow = [l for l in range(levels) if self.counts[l] > 1]
         self.wide = [l for l in range(levels) if self.counts[l] == 1]
         self.crossing = [l for l in range(levels) if self.groups[l] > 1]
-        self.padded = {l: round_up(self.counts[l], TILE) for l in self.narrow}
+        self.padded = {l: round_up(self.counts[l], TILE // 2) for l in self.narrow}
         self.offsets, at = {}, 0
         for l in self.narrow:
             self.offsets[l] = at
             at += kinds * self.padded[l]
         self.narrow_rows = at
+        self.small = [l for l in self.narrow if self.padded[l] % TILE]
+        self.cut = min([self.offsets[l] for l in self.small], default=at)
+        self.narrow_rows = round_up(at, 2 * TILE)
         self.wide_used = len(self.wide) * kinds + 2
         self.wide_rows = round_up(self.wide_used, TILE)
 
@@ -74,13 +77,11 @@
 def exchange_kernel(plan, segments, pattern_hbm, fine_hbm, restrict_hbm, inverse_hbm, stencil_hbm,
                     table_ref, level0_ref, spread_ref,
                     pattern_ref, fine_ref, restrict_ref, inverse_ref, stencil_ref, wide_f32, wide_onehot, onehot, few,
-                    grouped, joint, pair_weights, split, rows, coarse_ref, halo_ref, beside_ref,
-                    from_group, to_column, from_column, to_group, back,
+                    grouped, grouped_small, joint, pair_weights, split, rows, coarse_ref, own_ref, result_ref, halo_ref, beside_ref,
+                    from_group, to_column, early_ref, from_column, to_group, back,
                     fine_sem, weight_sem, group_send, group_recv,
-                    column_send, column_recv, back_send, back_recv, halo_send, halo_recv):
+                    early_send, early_recv, column_send, column_recv, back_send, back_recv, halo_send, halo_recv):
     width, kinds, blocks = plan.width, plan.kinds, plan.blocks
-    load = 16
-    loads = plan.vectors // load
     devices = plan.devices
     near = plan.groups[plan.crossing[0]]
     far = devices // near
@@ -88,12 +89,19 @@
     crossing = len(plan.crossing)
     part = plan.vectors // near
     me = lax.axis_index("gx")
+    early = me < 2
     mine = lax.rem(me, near)
     place = me // near
 
-    def fine_copy(step):
-        here = pl.ds(step * load, load)
-        return pltpu.make_async_copy(fine_hbm.at[here], fine_ref.at[here], fine_sem.at[step])
+    def part_of(index):
+        return pl.ds(pl.multiple_of(index * part, part), part)
+
+    def part_at(turn):
+        return lax.rem(mine + 1 + turn, near)
+
+    def fine_copy(turn):
+        here = part_of(part_at(turn))
+        return pltpu.make_async_copy(fine_hbm.at[here], fine_ref.at[here], fine_sem.at[turn])
 
     wide_first = plan.wide[0]
     wide_weights = pl.ds(wide_first, len(plan.wide))
@@ -105,10 +113,10 @@
     ]
     pattern_copy = pltpu.make_async_copy(pattern_hbm, pattern_ref, weight_sem.at[4])
     pattern_copy.start()
-    for step in range(loads - 1):
-        fine_copy(step).start()
+    for turn in range(near - 1):
+        fine_copy(turn).start()
     weight_copies[0].start()
-    fine_copy(loads - 1).start()
+    fine_copy(near - 1).start()
     for copy in weight_copies[1:]:
         copy.start()
 
@@ -136,51 +144,65 @@
         spread_ref[:, columns] = narrow_onehot(plan, turned, level, 1)
     spread_ref[:, pl.ds(plan.narrow_rows, plan.wide_rows)] = wide_rows_onehot(plan, turned, 1)
 
-    def extract(step):
-        for row in range(plan.wide_used):
-            rows[row, pl.ds(step * load, load), :] = few[step % 2, pl.ds(row, load, stride=PITCH), :].astype(BF16)
-
-    for step in range(loads):
-        fine_copy(step).wait()
-        for first in range(0, load, 2):
-            at = step * load + first
+    for row in range(plan.wide_used):
+        rows[row, part_of(mine), :] = jnp.zeros((part, width), BF16)
+
+    def gather(turn):
+        fine_copy(turn).wait()
+        for first in range(0, part, 2):
+            at = part_at(turn) * part + first
             both = jnp.concatenate([fine_ref[at], fine_ref[at + 1]], axis=1)
             both = jnp.dot(wide_onehot[...], both, preferred_element_type=F32)
-            few[step % 2, pl.ds(first * PITCH, plan.wide_rows), :] = both[:, :width]
-            few[step % 2, pl.ds((first + 1) * PITCH, plan.wide_rows), :] = both[:, width:]
-        if step > 0:
-            extract(step - 1)
-    extract(loads - 1)
+            few[turn % 2, pl.ds(first * PITCH, plan.wide_rows), :] = both[:, :width]
+            few[turn % 2, pl.ds((first + 1) * PITCH, plan.wide_rows), :] = both[:, width:]
+
+    def extract(turn):
+        for row in range(plan.wide_used):
+            rows[row, part_of(part_at(turn)), :] = few[turn % 2, pl.ds(row, part, stride=PITCH), :].astype(BF16)
+
+    def coarsen(position, vectors):
+        level, first = plan.wide[position], position * kinds
+        joined = jnp.concatenate([rows[first + kind, vectors, :] for kind in range(kinds)], axis=1)
+        coarse = jnp.dot(joined, restrict_ref[level], preferred_element_type=F32)
+        return coarse * plan.spans[level] ** (-0.5)
+
+    every = pl.ds(0, plan.vectors)
+    for turn in range(near - 1):
+        gather(turn)
+        if turn > 0:
+            extract(turn - 1)
+    extract(near - 2)
     weight_copies[0].wait()
-    for position, level in enumerate(plan.wide):
-        first = position * kinds
-        joined = jnp.concatenate([rows[first + kind] for kind in range(kinds)], axis=1)
-        coarse = jnp.dot(joined, restrict_ref[level], preferred_element_type=F32)
-        coarse_ref[position] = (coarse * plan.spans[level] ** (-0.5)).astype(BF16)
-    base = len(plan.wide) * kinds
-    halo_ref[0] = rows[base]
-    halo_ref[1] = rows[base + 1]
+    for index in range(crossing):
+        coarse_ref[index] = coarsen(local + index, every).astype(BF16)
 
     pl.semaphore_wait(barrier, len(peers))
-
-    def part_of(index):
-        return pl.ds(pl.multiple_of(index * part, part), part)
 
     copies = []
     for apart in range(1, near):
         theirs = lax.rem(mine + apart, near)
         copies.append(pltpu.make_async_remote_copy(
-            src_ref=coarse_ref.at[pl.ds(local, crossing), part_of(theirs), :],
+            src_ref=coarse_ref.at[:, part_of(theirs), :],
             dst_ref=from_group.at[apart],
             send_sem=group_send.at[apart], recv_sem=group_recv.at[apart],
             device_id=(group_peer(apart),), device_id_type=MESH))
+    for copy in copies:
+        copy.start()
+
+    gather(near - 1)
+    extract(near - 1)
+    for index in range(crossing):
+        own_ref[index] = coarsen(local + index, part_of(mine))
+    base = len(plan.wide) * kinds
+    halo_ref[0] = rows[base]
+    halo_ref[1] = rows[base + 1]
     halo_copies = []
     for side, peer in ((0, previous), (1, nexts)):
         halo_copies.append(pltpu.make_async_remote_copy(
             src_ref=halo_ref.at[side], dst_ref=beside_ref.at[1 - side],
             send_sem=halo_send.at[side], recv_sem=halo_recv.at[1 - side],
             device_id=(peer,), device_id_type=MESH))
-    for copy in copies + halo_copies:
+    for copy in halo_copies:
         copy.start()
 
     for copy in weight_copies[1:]:
@@ -203,9 +225,12 @@
         for slot in range(0, chunk, 2):
             at = start + slot
             both = jnp.concatenate([fine_ref[at], fine_ref[at + 1]], axis=1)
-            both = jnp.dot(onehot[...], both, preferred_element_type=F32).astype(BF16)
-            grouped[slot] = both[:, :width]
-            grouped[slot + 1] = both[:, width:]
+            both = jnp.dot(onehot[...], both, preferred_element_type=F32)
+            large = both[: plan.cut].astype(BF16)
+            grouped[slot] = large[:, :width]
+            grouped[slot + 1] = large[:, width:]
+            grouped_small[slot] = both[plan.cut :, :width]
+            grouped_small[slot + 1] = both[plan.cut :, width:]
         for slot in range(chunk):
             at = start + slot
             turn = slot % 4
@@ -219,13 +244,15 @@
             level0_ref[at, pl.ds(1, pairs, stride=2), :] = four[:, width : 2 * width] + later
         for position, level in enumerate(plan.narrow):
             padded = plan.padded[level]
-            slices = [pl.ds(plan.offsets[level] + kind * padded, padded) for kind in range(kinds)]
+            small = level in plan.small
+            source, first = (grouped_small, plan.cut) if small else (grouped, 0)
+            slices = [pl.ds(plan.offsets[level] - first + kind * padded, padded) for kind in range(kinds)]
             joined = jnp.concatenate(
-                [grouped[pl.ds(0, chunk), tile, :].reshape(chunk * padded, width) for tile in slices], axis=1)
-            lifted = jnp.dot(joined, joint[position], preferred_element_type=F32).astype(BF16)
-            for kind, tile in enumerate(slices):
-                table_ref[pl.ds(start, chunk), tile, :] = (
-                    lifted[:, kind * width : (kind + 1) * width].reshape(chunk, padded, width))
+                [source[pl.ds(0, chunk), tile, :].reshape(chunk * padded, width).astype(BF16) for tile in slices], axis=1)
+            lifted = jnp.dot(joined, joint[position], preferred_element_type=F32)
+            tiles = [lifted[:, kind * width : (kind + 1) * width].reshape(chunk, padded, width) for kind in range(kinds)]
+            target = pl.ds(plan.offsets[level], kinds * padded)
+            table_ref[pl.ds(start, chunk), target, :] = jnp.concatenate(tiles, axis=1).astype(BF16)
 
     def lift_wide(position, rounded):
         level = plan.wide[position]
@@ -239,7 +266,12 @@
     starts = [sum(segments[:index]) for index in range(len(segments))]
     narrow(starts[0], segments[0])
 
-    total = coarse_ref[pl.ds(local, crossing), part_of(mine), :].astype(F32)
+    @pl.when(early)
+    def _():
+        narrow(starts[1], segments[1])
+
+
+    total = own_ref[...]
     for apart, copy in enumerate(copies, 1):
         copy.wait_recv()
         total = total + from_group[apart].astype(F32)
@@ -251,7 +283,13 @@
             src_ref=to_column.at[pl.ds(1, crossing - 1)], dst_ref=from_column.at[apart],
             send_sem=column_send.at[apart], recv_sem=column_recv.at[apart],
             device_id=(column_peer(apart),), device_id_type=MESH))
-    for copy in column_copies:
+    early_copies = []
+    for apart in range(1, near):
+        early_copies.append(pltpu.make_async_remote_copy(
+            src_ref=to_column.at[0], dst_ref=early_ref.at[apart],
+            send_sem=early_send.at[apart], recv_sem=early_recv.at[apart],
+            device_id=(group_peer(apart),), device_id_type=MESH))
+    for copy in column_copies + early_copies:
         copy.start()
 
     for copy in halo_copies:
@@ -261,10 +299,9 @@
     wide_f32[pl.ds(base, plan.vectors, stride=PITCH), :] = jnp.dot(beside_ref[0], stencil_ref[0], preferred_element_type=F32)
     wide_f32[pl.ds(base + 1, plan.vectors, stride=PITCH), :] = jnp.dot(beside_ref[1], stencil_ref[2], preferred_element_type=F32)
     for position in range(local):
-        lift_wide(position, coarse_ref[position])
-    narrow(starts[1], segments[1])
-
-    to_group[0] = to_column[0]
+        lift_wide(position, coarsen(position, every).astype(BF16))
+    narrow(starts[2], segments[2])
+
     sums = [to_column[index].astype(F32) for index in range(crossing)]
     for apart, copy in enumerate(column_copies, 1):
         copy.wait_recv()
@@ -274,7 +311,7 @@
             keep = (source // reach == place // reach).astype(F32)
             sums[index] = sums[index] + keep * from_column[apart, index - 1].astype(F32)
     for index in range(1, crossing):
-        to_group[index] = sums[index].astype(BF16)
+        to_group[index - 1] = sums[index].astype(BF16)
 
     back_copies = []
     for apart in range(1, near):
@@ -285,20 +322,30 @@
     for copy in back_copies:
         copy.start()
 
-    narrow(starts[2], segments[2])
-    for copy in copies:
-        copy.wait_send()
-    coarse_ref[pl.ds(local, crossing), part_of(mine), :] = to_group[...]
+    result_ref[0, part_of(mine), :] = to_column[0]
+    for apart, copy in enumerate(early_copies, 1):
+        copy.wait_recv()
+        result_ref[0, part_of(lax.rem(mine + near - apart, near)), :] = early_ref[apart]
+    lift_wide(local, result_ref[0])
+
+    @pl.when(jnp.logical_not(early))
+    def _():
+        narrow(starts[1], segments[1])
+
+    narrow(starts[3], segments[3])
+    for index in range(1, crossing):
+        result_ref[index, part_of(mine), :] = to_group[index - 1]
     for apart, copy in enumerate(back_copies, 1):
         copy.wait_recv()
         source = lax.rem(mine + near - apart, near)
-        coarse_ref[pl.ds(local, crossing), part_of(source), :] = back[apart]
-    for position in range(local, len(plan.wide)):
-        lift_wide(position, coarse_ref[position])
+        for index in range(1, crossing):
+            result_ref[index, part_of(source), :] = back[apart, index - 1]
+    for index in range(1, crossing):
+        lift_wide(local + index, result_ref[index])
     for vector in range(plan.vectors):
         table_ref[vector, pl.ds(plan.narrow_rows, plan.wide_rows), :] = (
             wide_f32[pl.ds(vector * PITCH, plan.wide_rows), :].astype(BF16))
-    for copy in halo_copies + column_copies + back_copies:
+    for copy in copies + halo_copies + column_copies + early_copies + back_copies:
         copy.wait_send()
 
 
@@ -326,9 +373,8 @@
     levels, kinds = restrict.shape[:2]
     plan = Plan(devices, vectors, blocks, width, levels, kinds)
     stacked = restrict.reshape(levels, kinds * width, width)
-    wide_count = len(plan.wide)
-    some = vectors // 4
-    segments = (some, 2 * some, vectors - 3 * some)
+    eighth = vectors // 8
+    segments = (3 * eighth // 2, 2 * eighth, 3 * eighth, 3 * eighth // 2)
     near = plan.groups[plan.crossing[0]]
     far = devices // near
     crossing = len(plan.crossing)
@@ -356,22 +402,26 @@
             pltpu.VMEM((vectors * PITCH, width), F32),
             pltpu.VMEM((plan.wide_rows, blocks), BF16),
             pltpu.VMEM((plan.narrow_rows, blocks), BF16),
-            pltpu.VMEM((2, 16 * PITCH, width), F32),
-            pltpu.VMEM((max(segments), plan.narrow_rows, width), BF16),
+            pltpu.VMEM((2, part * PITCH, width), F32),
+            pltpu.VMEM((max(segments), plan.cut, width), BF16),
+            pltpu.VMEM((max(segments), plan.narrow_rows - plan.cut, width), F32),
             pltpu.VMEM((len(plan.narrow), kinds * width, kinds * width), BF16),
             pltpu.VMEM((2 * width, 4 * width), BF16),
             pltpu.VMEM((4, blocks, width), F32),
             pltpu.VMEM((plan.wide_used, vectors, width), BF16),
-            pltpu.VMEM((wide_count, vectors, width), BF16),
+            pltpu.VMEM((crossing, vectors, width), BF16),
+            pltpu.VMEM((crossing, part, width), F32),
+            pltpu.VMEM((crossing, vectors, width), BF16),
             pltpu.VMEM((2, vectors, width), BF16),
             pltpu.VMEM((2, vectors, width), BF16),
             pltpu.VMEM((near, crossing, part, width), BF16),
             pltpu.VMEM((crossing, part, width), BF16),
+            pltpu.VMEM((near, part, width), BF16),
             pltpu.VMEM((far, crossing - 1, part, width), BF16),
-            pltpu.VMEM((crossing, part, width), BF16),
-            pltpu.VMEM((near, crossing, part, width), BF16),
-            dma((vectors // 16,)), dma((5,)),
-            dma((near,)), dma((near,)), dma((far,)), dma((far,)), dma((near,)), dma((near,)), dma((2,)), dma((2,)),
+            pltpu.VMEM((crossing - 1, part, width), BF16),
+            pltpu.VMEM((near, crossing - 1, part, width), BF16),
+            dma((near,)), dma((5,)),
+            dma((near,)), dma((near,)), dma((near,)), dma((near,)), dma((far,)), dma((far,)), dma((near,)), dma((near,)), dma((2,)), dma((2,)),
         ],
         compiler_params=pltpu.CompilerParams(
             collective_id=0, has_side_effects=True, vmem_limit_bytes=VMEM_LIMIT),

time: 22.2 us -> 21.9 us (0.986)
  Pallas kernels: 22 us -> 21.5 us
    pallas_call x1, Pallas kernels: 18.2 us -> 17.7 us  [shards(): pl.pallas_call(functools.partial(exchange_kernel, plan, segments), out_sh...]
where the time goes in v4:
time: 21.9 us; the launch traced here: 21.7 us
  Pallas kernels  21.5 us (98%)
    pallas_call x1, Pallas kernels, shards(): pl.pallas_call(functools.partial(exchange_kernel, plan, segments), out_sh...  17.7 us
    pallas_call x1, Pallas kernels, shards(): pl.pallas_call(functools.partial(final_kernel, plan, pieces), out_shape=j...  3.76 us

profile of v4, /device:TPU:0, one launch (start us, length us, event | category | flops | bytes accessed | tf_op | source)
XLA Modules:
  0.0 21.7 jit_solution(768362568318443643)
XLA Ops:
  0.0 17.7 %exchange.1 = (bf16[64,384,128]{2,1,0:T(8,128)(2,1)S(1)}, f32[64,256,128]{2,1,0:T(8,128)S(1)}, bf16[256,384]{1,0:T(8,128)(2,1)S(1)}) custom-call(s32[8,256]{1,0:T(8,128)} %pattern_hbm.1, bf16[64,256,128]{2,1,0:T(8,128)(2,1)} %fine_hbm.1, bf16[8,512,128]{2,1,0:T(8,128)(2,1)} %bitcast.1, bf16[8,128,128]{2,1,0:T(8,128)(2,1)} %inverse_hbm.1, ...), custom_call_target="tpu_custom_call" | custom-call | tf_op jit(solution)/shard_map/exchange/pallas_call | solution.py:387
  17.7 3.8 %final.1 = f32[64,256,128]{2,1,0:T(8,128)} custom-call(bf16[256,384]{1,0:T(8,128)(2,1)S(1)} %get-tuple-element.8.spread_ref, bf16[64,384,128]{2,1,0:T(8,128)(2,1)S(1)} %get-tuple-element.9.table_ref, f32[64,256,128]{2,1,0:T(8,128)S(1)} %get-tuple-element.10.level0_ref), custom_call_target="tpu_custom_call" | custom-call | tf_op jit(solution)/shard_map/final/pallas_call | solution.py:432

commit v5 on v4

--- a/solution.py
+++ b/solution.py
@@ -43,19 +43,26 @@
         self.small = [l for l in self.narrow if self.padded[l] % TILE]
         self.cut = min([self.offsets[l] for l in self.small], default=at)
         self.narrow_rows = round_up(at, 2 * TILE)
-        self.wide_used = len(self.wide) * kinds + 2
-        self.wide_rows = round_up(self.wide_used, TILE)
+        early = len(self.wide) - len(self.crossing) + 1
+        self.base = early * kinds
+        self.late_first = round_up(self.base + 2, TILE)
+        late = self.late_first - self.base
+        self.wide_at = [p * kinds + (late if p >= early else 0) for p in range(len(self.wide))]
+        self.wide_end = self.wide_at[-1] + kinds
+        self.wide_rows = round_up(self.wide_end, 2 * TILE)
+        used = [at + kind for at in self.wide_at for kind in range(kinds)] + [self.base, self.base + 1]
+        self.wide_used = sorted(used)
 
 
 def wide_rows_onehot(plan, pattern, rows_axis):
     shape = (plan.wide_rows, plan.blocks) if rows_axis == 0 else (plan.blocks, plan.wide_rows)
     row = lax.broadcasted_iota(jnp.int32, shape, rows_axis)
     block = lax.broadcasted_iota(jnp.int32, shape, 1 - rows_axis)
-    base = len(plan.wide) * plan.kinds
+    base = plan.base
     hit = ((row == base) & (block == 0)) | ((row == base + 1) & (block == plan.blocks - 1))
     for position, level in enumerate(plan.wide):
         kinds = pattern[level : level + 1, :] if rows_axis == 0 else pattern[:, level : level + 1]
-        first = position * plan.kinds
+        first = plan.wide_at[position]
         inside = (row >= first) & (row < first + plan.kinds)
         hit = hit | (inside & (row - first == kinds))
     return hit.astype(F32).astype(BF16)
@@ -77,7 +84,7 @@
 def exchange_kernel(plan, segments, pattern_hbm, fine_hbm, restrict_hbm, inverse_hbm, stencil_hbm,
                     table_ref, level0_ref, spread_ref,
                     pattern_ref, fine_ref, restrict_ref, inverse_ref, stencil_ref, wide_f32, wide_onehot, onehot, few,
-                    grouped, grouped_small, joint, pair_weights, split, rows, coarse_ref, own_ref, result_ref, halo_ref, beside_ref,
+                    grouped, grouped_small, joint, joint_wide, pair_weights, split, rows, coarse_ref, own_ref, result_ref, halo_ref, beside_ref,
                     from_group, to_column, early_ref, from_column, to_group, back,
                     fine_sem, weight_sem, group_send, group_recv,
                     early_send, early_recv, column_send, column_recv, back_send, back_recv, halo_send, halo_recv):
@@ -144,7 +151,7 @@
         spread_ref[:, columns] = narrow_onehot(plan, turned, level, 1)
     spread_ref[:, pl.ds(plan.narrow_rows, plan.wide_rows)] = wide_rows_onehot(plan, turned, 1)
 
-    for row in range(plan.wide_used):
+    for row in plan.wide_used:
         rows[row, part_of(mine), :] = jnp.zeros((part, width), BF16)
 
     def gather(turn):
@@ -157,11 +164,11 @@
             few[turn % 2, pl.ds((first + 1) * PITCH, plan.wide_rows), :] = both[:, width:]
 
     def extract(turn):
-        for row in range(plan.wide_used):
+        for row in plan.wide_used:
             rows[row, part_of(part_at(turn)), :] = few[turn % 2, pl.ds(row, part, stride=PITCH), :].astype(BF16)
 
     def coarsen(position, vectors):
-        level, first = plan.wide[position], position * kinds
+        level, first = plan.wide[position], plan.wide_at[position]
         joined = jnp.concatenate([rows[first + kind, vectors, :] for kind in range(kinds)], axis=1)
         coarse = jnp.dot(joined, restrict_ref[level], preferred_element_type=F32)
         return coarse * plan.spans[level] ** (-0.5)
@@ -193,7 +200,7 @@
     extract(near - 1)
     for index in range(crossing):
         own_ref[index] = coarsen(local + index, part_of(mine))
-    base = len(plan.wide) * kinds
+    base = plan.base
     halo_ref[0] = rows[base]
     halo_ref[1] = rows[base + 1]
     halo_copies = []
@@ -256,11 +263,14 @@
 
     def lift_wide(position, rounded):
         level = plan.wide[position]
-        solved = jnp.dot(rounded, inverse_ref[level], preferred_element_type=F32).astype(BF16)
-        lifted = lax.dot_general(
-            solved, restrict_ref[level], (((1,), (1,)), ((), ())), preferred_element_type=F32)
+        if position > local:
+            lifted = jnp.dot(rounded, joint_wide[position - local - 1], preferred_element_type=F32)
+        else:
+            solved = jnp.dot(rounded, inverse_ref[level], preferred_element_type=F32).astype(BF16)
+            lifted = lax.dot_general(
+                solved, restrict_ref[level], (((1,), (1,)), ((), ())), preferred_element_type=F32)
         for kind in range(kinds):
-            wide_f32[pl.ds(position * kinds + kind, plan.vectors, stride=PITCH), :] = (
+            wide_f32[pl.ds(plan.wide_at[position] + kind, plan.vectors, stride=PITCH), :] = (
                 lifted[:, kind * width : (kind + 1) * width])
 
     starts = [sum(segments[:index]) for index in range(len(segments))]
@@ -294,10 +304,15 @@
 
     for copy in halo_copies:
         copy.wait_recv()
-    for row in range(plan.wide_used, plan.wide_rows):
+    for row in sorted(set(range(plan.wide_rows)) - set(plan.wide_used)):
         wide_f32[pl.ds(row, plan.vectors, stride=PITCH), :] = jnp.zeros((plan.vectors, width), F32)
     wide_f32[pl.ds(base, plan.vectors, stride=PITCH), :] = jnp.dot(beside_ref[0], stencil_ref[0], preferred_element_type=F32)
     wide_f32[pl.ds(base + 1, plan.vectors, stride=PITCH), :] = jnp.dot(beside_ref[1], stencil_ref[2], preferred_element_type=F32)
+    for index in range(1, crossing):
+        level = plan.crossing[index]
+        joint_wide[index - 1] = lax.dot_general(
+            inverse_ref[level], restrict_ref[level], (((1,), (1,)), ((), ())),
+            preferred_element_type=F32).astype(BF16)
     for position in range(local):
         lift_wide(position, coarsen(position, every).astype(BF16))
     narrow(starts[2], segments[2])
@@ -328,6 +343,13 @@
         result_ref[0, part_of(lax.rem(mine + near - apart, near)), :] = early_ref[apart]
     lift_wide(local, result_ref[0])
 
+    def fill(first, stop):
+        for vector in range(plan.vectors):
+            table_ref[vector, pl.ds(plan.narrow_rows + first, stop - first), :] = (
+                wide_f32[pl.ds(vector * PITCH + first, stop - first), :].astype(BF16))
+
+    fill(0, plan.late_first)
+
     @pl.when(jnp.logical_not(early))
     def _():
         narrow(starts[1], segments[1])
@@ -342,9 +364,7 @@
             result_ref[index, part_of(source), :] = back[apart, index - 1]
     for index in range(1, crossing):
         lift_wide(local + index, result_ref[index])
-    for vector in range(plan.vectors):
-        table_ref[vector, pl.ds(plan.narrow_rows, plan.wide_rows), :] = (
-            wide_f32[pl.ds(vector * PITCH, plan.wide_rows), :].astype(BF16))
+    fill(plan.late_first, plan.wide_rows)
     for copy in copies + halo_copies + column_copies + early_copies + back_copies:
         copy.wait_send()
 
@@ -406,9 +426,10 @@
             pltpu.VMEM((max(segments), plan.cut, width), BF16),
             pltpu.VMEM((max(segments), plan.narrow_rows - plan.cut, width), F32),
             pltpu.VMEM((len(plan.narrow), kinds * width, kinds * width), BF16),
+            pltpu.VMEM((crossing - 1, width, kinds * width), BF16),
             pltpu.VMEM((2 * width, 4 * width), BF16),
             pltpu.VMEM((4, blocks, width), F32),
-            pltpu.VMEM((plan.wide_used, vectors, width), BF16),
+            pltpu.VMEM((plan.wide_end, vectors, width), BF16),
             pltpu.VMEM((crossing, vectors, width), BF16),
             pltpu.VMEM((crossing, part, width), F32),
             pltpu.VMEM((crossing, vectors, width), BF16),
@@ -428,7 +449,7 @@
         name="exchange",
     )(*pinned)
 
-    pieces = [2, 2, 4] + [8] * (vectors // 8 - 2) + [4, 2, 2]
+    pieces = [4] * (vectors // 4)
     return pl.pallas_call(
         functools.partial(final_kernel, plan, pieces),
         out_shape=jax.ShapeDtypeStruct(fine.shape, F32),

time: 21.9 us -> 21.5 us (0.982)
  Pallas kernels: 21.5 us -> 21.1 us
    pallas_call x1, Pallas kernels: 17.7 us -> 17.4 us  [shards(): pl.pallas_call(functools.partial(exchange_kernel, plan, segments), out_sh...]
where the time goes in v5:
time: 21.5 us; the launch traced here: 21.3 us
  Pallas kernels  21.1 us (98%)
    pallas_call x1, Pallas kernels, shards(): pl.pallas_call(functools.partial(exchange_kernel, plan, segments), out_sh...  17.4 us
    pallas_call x1, Pallas kernels, shards(): pl.pallas_call(functools.partial(final_kernel, plan, pieces), out_shape=j...  3.72 us

profile of v5, /device:TPU:0, one launch (start us, length us, event | category | flops | bytes accessed | tf_op | source)
XLA Modules:
  0.0 21.3 jit_solution(640087565092683257)
XLA Ops:
  0.0 17.4 %exchange.1 = (bf16[64,384,128]{2,1,0:T(8,128)(2,1)S(1)}, f32[64,256,128]{2,1,0:T(8,128)S(1)}, bf16[256,384]{1,0:T(8,128)(2,1)S(1)}) custom-call(s32[8,256]{1,0:T(8,128)} %pattern_hbm.1, bf16[64,256,128]{2,1,0:T(8,128)(2,1)} %fine_hbm.1, bf16[8,512,128]{2,1,0:T(8,128)(2,1)} %bitcast.1, bf16[8,128,128]{2,1,0:T(8,128)(2,1)} %inverse_hbm.1, ...), custom_call_target="tpu_custom_call" | custom-call | tf_op jit(solution)/shard_map/exchange/pallas_call | solution.py:407
  17.4 3.7 %final.1 = f32[64,256,128]{2,1,0:T(8,128)} custom-call(bf16[256,384]{1,0:T(8,128)(2,1)S(1)} %get-tuple-element.8.spread_ref, bf16[64,384,128]{2,1,0:T(8,128)(2,1)S(1)} %get-tuple-element.9.table_ref, f32[64,256,128]{2,1,0:T(8,128)S(1)} %get-tuple-element.10.level0_ref), custom_call_target="tpu_custom_call" | custom-call | tf_op jit(solution)/shard_map/final/pallas_call | solution.py:453

commit v6 on v5

--- a/solution.py
+++ b/solution.py
@@ -394,7 +394,7 @@
     plan = Plan(devices, vectors, blocks, width, levels, kinds)
     stacked = restrict.reshape(levels, kinds * width, width)
     eighth = vectors // 8
-    segments = (3 * eighth // 2, 2 * eighth, 3 * eighth, 3 * eighth // 2)
+    segments = (eighth, 2 * eighth, 7 * eighth // 2, 3 * eighth // 2)
     near = plan.groups[plan.crossing[0]]
     far = devices // near
     crossing = len(plan.crossing)

time: 21.5 us -> 21.8 us (1.014)
  Pallas kernels: 21.1 us -> 21.4 us
    pallas_call x1, Pallas kernels: 17.4 us -> 17.7 us  [shards(): pl.pallas_call(functools.partial(exchange_kernel, plan, segments), out_sh...]
where the time goes in v6:
time: 21.8 us; the launch traced here: 21.6 us
  Pallas kernels  21.4 us (98%)
    pallas_call x1, Pallas kernels, shards(): pl.pallas_call(functools.partial(exchange_kernel, plan, segments), out_sh...  17.7 us
    pallas_call x1, Pallas kernels, shards(): pl.pallas_call(functools.partial(final_kernel, plan, pieces), out_shape=j...  3.72 us

profile of v6, /device:TPU:0, one launch (start us, length us, event | category | flops | bytes accessed | tf_op | source)
XLA Modules:
  0.0 21.6 jit_solution(13850184777522726060)
XLA Ops:
  0.0 17.7 %exchange.1 = (bf16[64,384,128]{2,1,0:T(8,128)(2,1)S(1)}, f32[64,256,128]{2,1,0:T(8,128)S(1)}, bf16[256,384]{1,0:T(8,128)(2,1)S(1)}) custom-call(s32[8,256]{1,0:T(8,128)} %pattern_hbm.1, bf16[64,256,128]{2,1,0:T(8,128)(2,1)} %fine_hbm.1, bf16[8,512,128]{2,1,0:T(8,128)(2,1)} %bitcast.1, bf16[8,128,128]{2,1,0:T(8,128)(2,1)} %inverse_hbm.1, ...), custom_call_target="tpu_custom_call" | custom-call | tf_op jit(solution)/shard_map/exchange/pallas_call | solution.py:407
  17.7 3.7 %final.1 = f32[64,256,128]{2,1,0:T(8,128)} custom-call(bf16[256,384]{1,0:T(8,128)(2,1)S(1)} %get-tuple-element.8.spread_ref, bf16[64,384,128]{2,1,0:T(8,128)(2,1)S(1)} %get-tuple-element.9.table_ref, f32[64,256,128]{2,1,0:T(8,128)S(1)} %get-tuple-element.10.level0_ref), custom_call_target="tpu_custom_call" | custom-call | tf_op jit(solution)/shard_map/final/pallas_call | solution.py:453
